TPU v7x, 768 devices: a whole 4x8x12 slice. The times are simulated.
768 devices in a mesh: az: 12 (over z_lo, x), rad: 64 (over y, z_hi, core).
Axes of the slice: x: 4, y: 8, z: 12 (z_hi: 4, z_lo: 3; z = z_hi * 3 + z_lo), core: 2. Of those that a mesh axis runs over, the one named last changes fastest.
Arguments:
- fields: float32 [5, 768, 32, 1536], P(None, 'rad', None, 'az'), may hold values from -6 to 6
- shift: int32 [768], replicated, may hold values from 0 to 1535
- fraction: float32 [768], replicated, may hold values from -0.5 to 0.5
- radial_rate: float32 [768, 32], replicated, may hold values from -0.4 to 0.4
Outputs:
- updated: float32 [5, 768, 32, 1536], P(None, 'rad', None, 'az')
All inputs are finite; a program needn't handle non-finite values.
Results may differ from a plain program's by a relative error of at most 0.0003.
Values sent between devices are 32-bit elements; how exact they have to be, the bound alone decides.
A program may use at most 64 MiB of HBM per device.

v0:
```python
import jax
import jax.numpy as jnp
from jax import lax
from jax.sharding import PartitionSpec as P


def split_up(array, dim, devices):
    before, after = (array.shape[:dim], array.shape[dim + 1 :])
    return jnp.moveaxis(array.reshape(*before, devices, -1, *after), dim, 0)


def cut_rows(length, count):
    lap = length // count
    if lap >= 8:
        lap -= lap % 8
    return [lap * k for k in range(1, count)]


def laid_out(pieces, dim):
    shape = list(pieces.shape[1:])
    shape[dim] *= pieces.shape[0]
    return jnp.moveaxis(pieces, 0, dim).reshape(shape)


def several_exchanges(array, axis, pieces, split_dim, concat_dim):
    blocks = split_up(array, split_dim, lax.axis_size(axis))
    widest = max(range(1, max(2, blocks.ndim - 1)), key=lambda d: blocks.shape[d])
    finished = []
    for section in jnp.split(blocks, cut_rows(blocks.shape[widest], pieces), axis=widest):
        if section.size:
            finished.append(lax.all_to_all(section, axis, split_axis=0, concat_axis=0, tiled=True))
    return laid_out(jnp.concatenate(finished, axis=widest), concat_dim)


def with_halo(array, sides, width):
    for axis, dim in sides:
        devices, length = (lax.axis_size(axis), array.shape[dim])
        up = [(i, (i + 1) % devices) for i in range(devices - 1)]
        down = [(j, i) for i, j in up]
        last = lax.slice_in_dim(array, length - width, length, axis=dim)
        first = lax.slice_in_dim(array, 0, width, axis=dim)
        before = lax.ppermute(last, axis, up)
        after = lax.ppermute(first, axis, down)
        array = jnp.concatenate([before, array, after], axis=dim)
    return array


def cut(values, low, count, axis):
    return lax.slice_in_dim(values, low, low + count, axis=axis)


def limited(left, right):
    steep = jnp.minimum(
        jnp.minimum(2.0 * jnp.abs(left), 2.0 * jnp.abs(right)), 0.5 * jnp.abs(left + right)
    )
    return jnp.where(left * right > 0.0, jnp.sign(left) * steep, 0.0)


def flux_change(padded, courant, axis):
    count = padded.shape[axis] - 4
    left = cut(padded, 1, count + 2, axis) - cut(padded, 0, count + 2, axis)
    right = cut(padded, 2, count + 2, axis) - cut(padded, 1, count + 2, axis)
    slope = limited(left, right)
    forward = cut(padded, 1, count + 1, axis) + 0.5 * (1.0 - courant) * cut(
        slope, 0, count + 1, axis
    )
    backward = cut(padded, 2, count + 1, axis) - 0.5 * (1.0 + courant) * cut(
        slope, 1, count + 1, axis
    )
    flux = courant * jnp.where(courant > 0.0, forward, backward)
    return cut(flux, 1, count, axis) - cut(flux, 0, count, axis)


def slice_rows(doubled, starts, length):

    def one_row(row, begin):
        return lax.dynamic_slice_in_dim(row, begin, length, axis=2)

    return jax.vmap(one_row, in_axes=(1, 0), out_axes=1)(doubled, starts)


def shards(fields, shift, fraction, radial_rate):
    rows_here = fields.shape[1]
    start = lax.axis_index("rad") * rows_here
    local_shift = lax.dynamic_slice_in_dim(shift, start, rows_here)
    local_fraction = lax.dynamic_slice_in_dim(fraction, start, rows_here)
    group = lax.axis_size("az")
    per_device = rows_here // group
    offset = lax.axis_index("az") * per_device
    row_shift = lax.dynamic_slice_in_dim(local_shift, offset, per_device)
    row_fraction = lax.dynamic_slice_in_dim(local_fraction, offset, per_device)
    block = lax.all_to_all(fields, "az", split_axis=1, concat_axis=3, tiled=True)
    cycle = block.shape[3]
    doubled = jnp.concatenate([block, block], axis=3)
    rolled = slice_rows(doubled, cycle - row_shift, cycle)
    padded = jnp.concatenate([rolled[:, :, :, -2:], rolled, rolled[:, :, :, :2]], axis=3)
    result = rolled - flux_change(padded, row_fraction[None, :, None, None], 3)
    azimuthal = several_exchanges(result, "az", 2, 3, 1)
    edge = jnp.zeros((1, radial_rate.shape[1]), jnp.float32)
    extended = jnp.concatenate([edge, radial_rate[:-1], edge], axis=0)
    face_rates = lax.dynamic_slice_in_dim(extended, start, rows_here + 1)
    ghosted = with_halo(azimuthal, (("rad", 1),), 2)
    return azimuthal - flux_change(ghosted, face_rates[None, :, :, None], 1)


def solution(mesh):
    placed = (P(None, "rad", None, "az"), P(), P(), P())
    return jax.shard_map(
        shards, mesh=mesh, in_specs=placed, out_specs=P(None, "rad", None, "az"), check_vma=False
    )
```

profile of v0, /device:TPU:7, one launch (start us, length us, event | category | flops | bytes accessed | tf_op | source)
XLA Modules:
  0.0 92.1 jit_solution(5869389908404080393)
XLA Ops:
  0.0 2.2 %copy.26 = f32[5,12,32,128]{3,2,0,1:T(8,128)} copy(f32[5,12,32,128]{3,2,1,0:T(8,128)} %param.4) | data formatting | bytes 1966080 | tf_op args[0]
  2.2 7.8 %all-to-all-start = ((f32[5,12,32,128]{3,2,0,1:T(8,128)}), f32[5,12,32,128]{3,2,0,1:T(8,128)S(1)}, u32[]{:S(2)}, u32[]{:S(2)}) async-start(f32[5,12,32,128]{3,2,0,1:T(8,128)} %copy.26), calls=%async_computation | async-start | bytes 1966080 | tf_op jit(solution)/shard_map/all_to_all | solution.py:92
  10.0 1.3 %dynamic_slice.15 = f32[1]{0:T(128)} dynamic-slice(f32[768]{0:T(1024)} %param.6, s32[]{:T(128)S(6)} %dynamic_slice.13), dynamic_slice_sizes={1} | dynamic-slice | bytes 12 | tf_op jit(solution)/shard_map/dynamic_slice | solution.py:91
  13.3 1.3 %dynamic_slice.14 = s32[1]{0:T(128)} dynamic-slice(s32[768]{0:T(1024)} %param.5, s32[]{:T(128)S(6)} %dynamic_slice.13), dynamic_slice_sizes={1} | dynamic-slice | bytes 12 | tf_op jit(solution)/shard_map/dynamic_slice | solution.py:90
  15.8 6.3 %all-to-all-done = f32[5,12,32,128]{3,2,0,1:T(8,128)S(1)} async-done(((f32[5,12,32,128]{3,2,0,1:T(8,128)}), f32[5,12,32,128]{3,2,0,1:T(8,128)S(1)}, u32[]{:S(2)}, u32[]{:S(2)}) %all-to-all-start) | async-done | bytes 983072 | tf_op jit(solution)/shard_map/all_to_all | solution.py:92
  22.1 0.1 copy_bitcast_fusion
  22.3 0.6 fusion.16
  22.8 0.1 fusion.23
  22.9 0.7 concatenate.37
  23.7 0.9 multiply_select_fusion.1
  24.6 1.3 %fusion.12 = f32[5,1,32,1537]{3,2,0,1:T(8,128)S(1)} fusion(f32[5,1,32,2]{3,2,0,1:T(8,128)S(1)} %get-tuple-element.21, f32[5,1,32,2]{3,2,0,1:T(8,128)S(1)} %get-tuple-element.20, f32[5,1,32,1538]{3,2,0,1:T(8,128)S(1)} %multiply_select_fusion.1, f32[5,1,32,1536]{3,2,0,1:T(8,128)S(1)} %fusion.16, f32[]{:T(128)} %bitcast.6, f32[]{:T(128)} %bitcast.5, ...), kind=kLoop, calls=%fused_computation.28 | loop fusion | flops 1967360 | bytes 3936653 | tf_op jit(solution)/shard_map/mul | solution.py:70
  25.9 0.9 fusion.18
  26.7 0.2 reshape.37
  26.9 0.1 fusion.21
  27.0 0.9 %copy.28 = f32[12,5,1,16,128]{4,3,2,1,0:T(8,128)} copy(f32[12,5,1,16,128]{4,0,3,1,2:T(8,128)S(1)} %get-tuple-element.16) | data formatting | bytes 983040 | tf_op jit(solution)/shard_map/split | solution.py:29
  28.0 7.9 %all-to-all-start.1 = ((f32[12,5,1,16,128]{4,3,2,1,0:T(8,128)}), f32[12,5,1,16,128]{4,3,2,1,0:T(8,128)S(1)}, u32[]{:S(2)}, u32[]{:S(2)}) async-start(f32[12,5,1,16,128]{4,3,2,1,0:T(8,128)} %copy.28), calls=%async_computation.1 | async-start | bytes 983040 | tf_op jit(solution)/shard_map/all_to_all | solution.py:31
  35.8 0.0 copy-start
  35.8 0.9 %copy.29 = f32[12,5,1,16,128]{4,3,2,1,0:T(8,128)} copy(f32[12,5,1,16,128]{4,0,3,1,2:T(8,128)S(1)} %get-tuple-element.17) | data formatting | bytes 983040 | tf_op jit(solution)/shard_map/split | solution.py:29
  36.8 7.2 %all-to-all-done.1 = f32[12,5,1,16,128]{4,3,2,1,0:T(8,128)S(1)} async-done(((f32[12,5,1,16,128]{4,3,2,1,0:T(8,128)}), f32[12,5,1,16,128]{4,3,2,1,0:T(8,128)S(1)}, u32[]{:S(2)}, u32[]{:S(2)}) %all-to-all-start.1) | async-done | bytes 491552 | tf_op jit(solution)/shard_map/all_to_all | solution.py:31
  43.9 4.0 %all-to-all-start.2 = ((f32[12,5,1,16,128]{4,3,2,1,0:T(8,128)}), f32[12,5,1,16,128]{4,3,2,1,0:T(8,128)S(1)}, u32[]{:S(2)}, u32[]{:S(2)}) async-start(f32[12,5,1,16,128]{4,3,2,1,0:T(8,128)} %copy.29), calls=%async_computation.2 | async-start | bytes 983040 | tf_op jit(solution)/shard_map/all_to_all | solution.py:31
  47.9 0.0 copy-done
  47.9 0.1 fusion.20
  48.0 0.1 copy.32
  48.1 7.6 %all-to-all-done.2 = f32[12,5,1,16,128]{4,3,2,1,0:T(8,128)S(1)} async-done(((f32[12,5,1,16,128]{4,3,2,1,0:T(8,128)}), f32[12,5,1,16,128]{4,3,2,1,0:T(8,128)S(1)}, u32[]{:S(2)}, u32[]{:S(2)}) %all-to-all-start.2) | async-done | bytes 491552 | tf_op jit(solution)/shard_map/all_to_all | solution.py:31
  55.6 0.1 maximum_bitcast_fusion
  55.8 22.1 %collective-permute-start = (f32[5,2,32,128]{3,2,0,1:T(8,128)S(1)}, f32[5,2,32,128]{3,2,0,1:T(8,128)S(1)}, u32[]{:S(2)}, u32[]{:S(2)}) collective-permute-start(f32[5,2,32,128]{3,2,0,1:T(8,128)S(1)} %get-tuple-element.18), channel_id=1, source_target_pairs={{0,1},{1,2},{2,3},{3,4},{4,5},{5,6},{6,7},{7,8},{8,9},{9,10},{10,1... | collective-permute-start | bytes 491528 | tf_op jit(solution)/shard_map/ppermute | solution.py:42
  77.8 1.9 %collective-permute-start.1 = (f32[5,2,32,128]{3,2,0,1:T(8,128)S(1)}, f32[5,2,32,128]{3,2,0,1:T(8,128)S(1)}, u32[]{:S(2)}, u32[]{:S(2)}) collective-permute-start(f32[5,2,32,128]{3,2,0,1:T(8,128)S(1)} %get-tuple-element.19), channel_id=1, source_target_pairs={{1,0},{2,1},{3,2},{4,3},{5,4},{6,5},{7,6},{8,7},{9,8},{10,9},{11,1... | collective-permute-start | bytes 491528 | tf_op jit(solution)/shard_map/ppermute | solution.py:43
  79.8 2.0 %collective-permute-done = f32[5,2,32,128]{3,2,0,1:T(8,128)S(1)} collective-permute-done((f32[5,2,32,128]{3,2,0,1:T(8,128)S(1)}, f32[5,2,32,128]{3,2,0,1:T(8,128)S(1)}, u32[]{:S(2)}, u32[]{:S(2)}) %collective-permute-start) | collective-permute-done | bytes 163872 | tf_op jit(solution)/shard_map/ppermute | solution.py:42
  81.8 8.0 %collective-permute-done.1 = f32[5,2,32,128]{3,2,0,1:T(8,128)S(1)} collective-permute-done((f32[5,2,32,128]{3,2,0,1:T(8,128)S(1)}, f32[5,2,32,128]{3,2,0,1:T(8,128)S(1)}, u32[]{:S(2)}, u32[]{:S(2)}) %collective-permute-start.1) | collective-permute-done | bytes 163872 | tf_op jit(solution)/shard_map/ppermute | solution.py:43
  89.8 0.7 multiply_select_fusion
  90.5 0.4 fusion.5
  90.9 0.2 fusion.17
  91.1 1.0 %copy.31 = f32[5,12,32,128]{3,2,1,0:T(8,128)} copy(f32[5,12,32,128]{3,2,0,1:T(8,128)S(1)} %fusion.17) | data formatting | bytes 1966080 | tf_op jit(solution)/shard_map/sub | solution.py:103
  (4 shorter events, 0.0 us)
Async XLA Ops:
  2.2 19.9 %all-to-all-start = ((f32[5,12,32,128]{3,2,0,1:T(8,128)}), f32[5,12,32,128]{3,2,0,1:T(8,128)S(1)}, u32[]{:S(2)}, u32[]{:S(2)}) async-start(f32[5,12,32,128]{3,2,0,1:T(8,128)} %copy.26), calls=%async_computation | async-start | bytes 1966080 | tf_op jit(solution)/shard_map/all_to_all | solution.py:92
  28.0 15.9 %all-to-all-start.1 = ((f32[12,5,1,16,128]{4,3,2,1,0:T(8,128)}), f32[12,5,1,16,128]{4,3,2,1,0:T(8,128)S(1)}, u32[]{:S(2)}, u32[]{:S(2)}) async-start(f32[12,5,1,16,128]{4,3,2,1,0:T(8,128)} %copy.28), calls=%async_computation.1 | async-start | bytes 983040 | tf_op jit(solution)/shard_map/all_to_all | solution.py:31
  35.8 12.0 %copy-start = (f32[768,32]{0,1:T(8,128)S(1)}, f32[768,32]{0,1:T(8,128)}, u32[]{:S(2)}) copy-start(f32[768,32]{0,1:T(8,128)} %param.7) | copy-start | bytes 294916
  43.9 11.7 %all-to-all-start.2 = ((f32[12,5,1,16,128]{4,3,2,1,0:T(8,128)}), f32[12,5,1,16,128]{4,3,2,1,0:T(8,128)S(1)}, u32[]{:S(2)}, u32[]{:S(2)}) async-start(f32[12,5,1,16,128]{4,3,2,1,0:T(8,128)} %copy.29), calls=%async_computation.2 | async-start | bytes 983040 | tf_op jit(solution)/shard_map/all_to_all | solution.py:31
  55.8 26.0 %collective-permute-start = (f32[5,2,32,128]{3,2,0,1:T(8,128)S(1)}, f32[5,2,32,128]{3,2,0,1:T(8,128)S(1)}, u32[]{:S(2)}, u32[]{:S(2)}) collective-permute-start(f32[5,2,32,128]{3,2,0,1:T(8,128)S(1)} %get-tuple-element.18), channel_id=1, source_target_pairs={{0,1},{1,2},{2,3},{3,4},{4,5},{5,6},{6,7},{7,8},{8,9},{9,10},{10,1... | collective-permute-start | bytes 491528 | tf_op jit(solution)/shard_map/ppermute | solution.py:42
  77.8 11.9 %collective-permute-start.1 = (f32[5,2,32,128]{3,2,0,1:T(8,128)S(1)}, f32[5,2,32,128]{3,2,0,1:T(8,128)S(1)}, u32[]{:S(2)}, u32[]{:S(2)}) collective-permute-start(f32[5,2,32,128]{3,2,0,1:T(8,128)S(1)} %get-tuple-element.19), channel_id=1, source_target_pairs={{1,0},{2,1},{3,2},{4,3},{5,4},{6,5},{7,6},{8,7},{9,8},{10,9},{11,1... | collective-permute-start | bytes 491528 | tf_op jit(solution)/shard_map/ppermute | solution.py:43
where the time goes:
time: 93.1 us; the launch traced here: 92.1 us
  starting transfers between devices  43.6 us (47%)
  waiting for transfers between devices  31 us (33%)
  local copies, waits for them, and re-layouts  8.99 us (10%)
  other arithmetic  5.1 us (5%)
  between operations  3.32 us (4%)
    ppermute x1, starting transfers between devices, with_halo(): before = lax.ppermute(last, axis, up)  22.1 us
    all_to_all x2, waiting for transfers between devices, several_exchanges(): lax.all_to_all(section, axis, split_axis=0, concat_axis=0, tiled=True)  14.7 us
    all_to_all x2, starting transfers between devices, several_exchanges(): lax.all_to_all(section, axis, split_axis=0, concat_axis=0, tiled=True)  11.8 us
    ppermute x1, waiting for transfers between devices, with_halo(): after = lax.ppermute(first, axis, down)  7.98 us
    all_to_all x1, starting transfers between devices, shards(): lax.all_to_all(fields, 'az', split_axis=1, concat_axis=3, tiled=True)  7.84 us
    all_to_all x1, waiting for transfers between devices, shards(): lax.all_to_all(fields, 'az', split_axis=1, concat_axis=3, tiled=True)  6.32 us
    unnamed x4, local copies, waits for them, and re-layouts  2.29 us
    ppermute x1, waiting for transfers between devices, with_halo(): before = lax.ppermute(last, axis, up)  2.02 us
  transfers between devices with their start and end apart: 5, of which 5 were waited for; matrix products, arithmetic and copies ran while one was open for 4% of the time, Pallas kernels for 0%

commit v1 on v0

v1 whole, which is shorter than its diff:
```python
import functools

import jax
import jax.numpy as jnp
from jax import lax
from jax.experimental import pallas as pl
from jax.experimental.pallas import tpu as pltpu
from jax.sharding import PartitionSpec as P

MESH = pl.DeviceIdType.MESH
LANES = 128
SUB = 8


def limited(left, right):
    steep = jnp.minimum(
        jnp.minimum(2.0 * jnp.abs(left), 2.0 * jnp.abs(right)), 0.5 * jnp.abs(left + right)
    )
    return jnp.where(left * right > 0.0, jnp.where(left > 0.0, steep, -steep), 0.0)


def blocks_back(x):
    return jnp.concatenate([x[-1:], x[:-1]], axis=0)


def blocks_on(x):
    return jnp.concatenate([x[1:], x[:1]], axis=0)


def kernel(
    n,
    groups,
    shift_ref,
    fraction_ref,
    fields_ref,
    rate_ref,
    out_ref,
    mine,
    whole,
    turned,
    rolled,
    tall,
    result,
    rate_raw,
    face_rate,
    load_sem,
    rate_sem,
    send_sem,
    gather_sem,
    row_sem,
    halo_send_sem,
    halo_sem,
    store_sem,
):
    nf, rows, polar, _ = mine.shape
    me = lax.axis_index("az")
    band = lax.axis_index("rad")
    first, last = band == 0, band == groups - 1

    for f in range(nf):
        pltpu.make_async_copy(fields_ref.at[f], mine.at[f], load_sem.at[f]).start()
    raw_rows = rate_raw.shape[0]
    low = jnp.maximum(band * rows - 1, 0) // SUB * SUB
    low = pl.multiple_of(jnp.minimum(low, groups * rows - raw_rows), SUB)
    rate_copy = pltpu.make_async_copy(rate_ref.at[pl.ds(low, raw_rows)], rate_raw, rate_sem)
    rate_copy.start()

    barrier = pltpu.get_barrier_semaphore()

    @pl.loop(1, n)
    def _(d):
        pl.semaphore_signal(
            barrier, inc=1, device_id={"az": lax.rem(me + d, n)}, device_id_type=MESH
        )

    @pl.when(jnp.logical_not(first))
    def _():
        pl.semaphore_signal(barrier, inc=1, device_id={"rad": band - 1}, device_id_type=MESH)

    @pl.when(jnp.logical_not(last))
    def _():
        pl.semaphore_signal(barrier, inc=1, device_id={"rad": band + 1}, device_id_type=MESH)

    inner = jnp.where(first, 0, 1) + jnp.where(last, 0, 1)
    pl.semaphore_wait(barrier, n - 1 + inner)

    for f in range(nf):
        pltpu.make_async_copy(fields_ref.at[f], mine.at[f], load_sem.at[f]).wait()

        @pl.loop(1, n)
        def _(d):
            to = lax.rem(me + d, n)
            pltpu.make_async_remote_copy(
                src_ref=mine.at[f, to],
                dst_ref=whole.at[f, me],
                send_sem=send_sem.at[0],
                recv_sem=gather_sem.at[f],
                device_id={"az": to},
                device_id_type=MESH,
            ).start()

    rate_copy.wait()
    at_lane = lax.broadcasted_iota(jnp.int32, (polar, polar), 1)
    at_sub = lax.broadcasted_iota(jnp.int32, (polar, polar), 0)
    for i in range(rows + 1):
        here = jnp.maximum(band * rows + i - 1, 0) - low
        line = rate_raw[pl.ds(here, 1), :]
        spread = jnp.where(at_lane == at_sub, jnp.broadcast_to(line, (polar, polar)), 0.0)
        column = jnp.sum(spread, axis=1, keepdims=True)
        if i == 0:
            column = jnp.where(first, 0.0, column)
        if i == rows:
            column = jnp.where(last, 0.0, column)
        face_rate[i] = jnp.broadcast_to(column, (polar, LANES))

    @pl.when(first)
    def _():
        tall[:, 0:2] = jnp.zeros((nf, 2, polar, LANES), jnp.float32)

    @pl.when(last)
    def _():
        tall[:, rows + 2 : rows + 4] = jnp.zeros((nf, 2, polar, LANES), jnp.float32)

    row = band * rows + me
    amount = shift_ref[row]
    courant = fraction_ref[row]
    blocks = amount >> 7
    lanes = amount & (LANES - 1)
    upwind = courant > 0.0
    weight = jnp.where(upwind, 0.5 * (1.0 - courant), -0.5 * (1.0 + courant))
    step = jnp.where(upwind, 1, LANES - 1)
    edge = jnp.where(upwind, 0, LANES - 1)
    lane = lax.broadcasted_iota(jnp.int32, (n, SUB, LANES), 2)
    lane_row = lax.broadcasted_iota(jnp.int32, (polar, LANES), 1)

    @pl.loop(0, nf)
    def _(f):
        whole[f, me] = mine[f, me]
        got = whole.at[f, pl.ds(0, n - 1)]
        pltpu.make_async_copy(got, got, gather_sem.at[f]).wait()

        for t in range(0, polar, SUB):
            q = whole[f, :, t : t + SUB, :]
            ahead = pltpu.roll(q, LANES - 1, 2)
            right = jnp.where(lane == LANES - 1, blocks_on(ahead), ahead) - q
            back = pltpu.roll(right, 1, 2)
            left = jnp.where(lane == 0, blocks_back(back), back)
            flux = courant * (q + weight * limited(left, right))
            other = pltpu.roll(flux, step, 2)
            beside = jnp.where(upwind, blocks_back(other), blocks_on(other))
            other = jnp.where(lane == edge, beside, other)
            change = jnp.where(upwind, flux - other, other - flux)
            turned[:, t : t + SUB, :] = pltpu.roll(q - change, lanes, 2)

        @pl.loop(0, n)
        def _(j):
            from_here = lax.rem(j - blocks + n, n)
            from_last = lax.rem(j - blocks - 1 + n + n, n)
            rolled[f, j] = jnp.where(lane_row >= lanes, turned[from_here], turned[from_last])

        @pl.loop(1, n)
        def _(d):
            to = lax.rem(me + d, n)
            pltpu.make_async_remote_copy(
                src_ref=rolled.at[f, to],
                dst_ref=tall.at[f, me + 2],
                send_sem=send_sem.at[1],
                recv_sem=row_sem.at[f, me],
                device_id={"az": to},
                device_id_type=MESH,
            ).start()

        tall[f, me + 2] = rolled[f, me]

    def await_row(f, j):
        @pl.when(me != j)
        def _():
            got = tall.at[f, j + 2]
            pltpu.make_async_copy(got, got, row_sem.at[f, j]).wait()

    def halo(f, up):
        src, dst, to = (rows, 0, band + 1) if up else (2, rows + 2, band - 1)
        return pltpu.make_async_remote_copy(
            src_ref=tall.at[f, pl.ds(src, 2)],
            dst_ref=tall.at[f, pl.ds(dst, 2)],
            send_sem=halo_send_sem.at[f, int(up)],
            recv_sem=halo_sem.at[f, int(up)],
            device_id={"rad": to},
            device_id_type=MESH,
        )

    def pass_on(f):
        await_row(f, 0)
        await_row(f, 1)
        await_row(f, rows - 2)
        await_row(f, rows - 1)

        @pl.when(jnp.logical_not(first))
        def _():
            halo(f, False).start()

        @pl.when(jnp.logical_not(last))
        def _():
            halo(f, True).start()

    def radial(f):
        for j in range(2, rows - 2):
            await_row(f, j)

        @pl.when(jnp.logical_not(first))
        def _():
            halo(f, True).wait_recv()

        @pl.when(jnp.logical_not(last))
        def _():
            halo(f, False).wait_recv()

        @pl.loop(0, polar // SUB)
        def _(i):
            t = pl.ds(pl.multiple_of(i * SUB, SUB), SUB)
            q = tall[f, :, t, :]
            c = face_rate[:, t, :]
            diff = q[1:] - q[:-1]
            slope = limited(diff[:-1], diff[1:])
            forward = q[1:-2] + 0.5 * (1.0 - c) * slope[:-1]
            backward = q[2:-1] - 0.5 * (1.0 + c) * slope[1:]
            flux = c * jnp.where(c > 0.0, forward, backward)
            result[f, :, t, :] = q[2:-2] - (flux[1:] - flux[:-1])

        pltpu.make_async_copy(result.at[f], out_ref.at[f], store_sem.at[f]).start()

    pass_on(0)

    @pl.loop(1, nf)
    def _(f):
        pass_on(f)
        radial(f - 1)

    radial(nf - 1)

    sent = whole.at[:, pl.ds(0, n - 1)]
    for phase in range(2):
        pltpu.make_async_copy(sent, sent, send_sem.at[phase]).wait()
    for f in range(nf):

        @pl.when(jnp.logical_not(first))
        def _():
            halo(f, False).wait_send()

        @pl.when(jnp.logical_not(last))
        def _():
            halo(f, True).wait_send()

        pltpu.make_async_copy(result.at[f], out_ref.at[f], store_sem.at[f]).wait()


def shards(n, groups, fields, shift, fraction, radial_rate):
    nf, rows, polar, lanes = fields.shape
    assert rows == n and lanes == LANES
    block = lambda *shape: pltpu.VMEM(shape, jnp.float32)
    return pl.pallas_call(
        functools.partial(kernel, n, groups),
        out_shape=jax.ShapeDtypeStruct(fields.shape, jnp.float32),
        in_specs=[
            pl.BlockSpec(memory_space=pltpu.SMEM),
            pl.BlockSpec(memory_space=pltpu.SMEM),
            pl.BlockSpec(memory_space=pl.ANY),
            pl.BlockSpec(memory_space=pl.ANY),
        ],
        out_specs=pl.BlockSpec(memory_space=pl.ANY),
        scratch_shapes=[
            block(nf, rows, polar, LANES),
            block(nf, n, polar, LANES),
            block(n, polar, LANES),
            block(nf, n, polar, LANES),
            block(nf, rows + 4, polar, LANES),
            block(nf, rows, polar, LANES),
            block(min(24, groups * rows), polar),
            block(rows + 1, polar, LANES),
            pltpu.SemaphoreType.DMA((nf,)),
            pltpu.SemaphoreType.DMA,
            pltpu.SemaphoreType.DMA((2,)),
            pltpu.SemaphoreType.DMA((nf,)),
            pltpu.SemaphoreType.DMA((nf, rows)),
            pltpu.SemaphoreType.DMA((nf, 2)),
            pltpu.SemaphoreType.DMA((nf, 2)),
            pltpu.SemaphoreType.DMA((nf,)),
        ],
        compiler_params=pltpu.CompilerParams(collective_id=0, has_side_effects=True),
        name="orbital",
    )(shift, fraction, fields, radial_rate)


def solution(mesh):
    placed = (P(None, "rad", None, "az"), P(), P(), P())
    body = functools.partial(shards, mesh.shape["az"], mesh.shape["rad"])
    return jax.shard_map(
        body, mesh=mesh, in_specs=placed, out_specs=P(None, "rad", None, "az"), check_vma=False
    )
```

time: 93.1 us -> 65 us (0.70)
  the two profiles are of different devices: /device:TPU:7 before, /device:TPU:32 now
where the time goes in v1:
time: 65 us; the launch traced here: 64.8 us
  Pallas kernels  60.7 us (93%)
  local copies, waits for them, and re-layouts  4.05 us (6%)
    pallas_call x1, Pallas kernels, shards(): pl.pallas_call(functools.partial(kernel, n, groups), out_shape=jax.ShapeD...  60.7 us
    unnamed x2, local copies, waits for them, and re-layouts  4.05 us

profile of v1, /device:TPU:32, one launch (start us, length us, event | category | flops | bytes accessed | tf_op | source)
XLA Modules:
  0.0 64.8 jit_solution(17391384304296883040)
XLA Ops:
  0.0 1.8 %copy.5.rate_ref = f32[768,32]{1,0:T(8,128)} copy(f32[768,32]{0,1:T(8,128)} %param.7) | data formatting | bytes 196608 | tf_op args[3]
  1.8 60.7 %orbital.1 = f32[5,12,32,128]{3,2,1,0:T(8,128)} custom-call(s32[768]{0:T(1024)} %shift_ref.1, f32[768]{0:T(1024)} %fraction_ref.1, f32[5,12,32,128]{3,2,1,0:T(8,128)} %fields_ref.1, f32[768,32]{1,0:T(8,128)} %copy.5.rate_ref), custom_call_target="tpu_custom_call" | custom-call | tf_op jit(solution)/shard_map/orbital/pallas_call | solution.py:261
  62.5 2.2 %copy.7 = f32[5,12,32,128]{3,2,1,0:T(8,128)} copy(f32[5,12,32,128]{3,2,1,0:T(8,128)} %orbital.1) | data formatting | bytes 1966080

commit v2 on v1

v2 whole, which is shorter than its diff:
```python
import functools

import jax
import jax.numpy as jnp
from jax import lax
from jax.experimental import pallas as pl
from jax.experimental.pallas import tpu as pltpu
from jax.sharding import PartitionSpec as P

MESH = pl.DeviceIdType.MESH
LANES = 128
SUB = 8
AHEAD = 3
VMEM_BYTES = 67043328 - 6000000


def limited(left, right):
    steep = jnp.minimum(
        jnp.minimum(2.0 * jnp.abs(left), 2.0 * jnp.abs(right)), 0.5 * jnp.abs(left + right)
    )
    return jnp.where(left * right > 0.0, jnp.where(left > 0.0, steep, -steep), 0.0)


def blocks_back(x):
    return jnp.concatenate([x[-1:], x[:-1]], axis=0)


def blocks_on(x):
    return jnp.concatenate([x[1:], x[:1]], axis=0)


def kernel(
    n,
    groups,
    shift_ref,
    fraction_ref,
    fields_ref,
    rate_ref,
    out_ref,
    mine,
    whole,
    turned,
    rolled,
    tall,
    shift_smem,
    fraction_smem,
    rate_raw,
    face_rate,
    load_sem,
    rate_sem,
    send_sem,
    gather_sem,
    row_sem,
    halo_send_sem,
    halo_sem,
    go_sem,
    met_sem,
    scalar_sem,
):
    nf, rows, polar, _ = mine.shape
    me = lax.axis_index("az")
    band = lax.axis_index("rad")
    first, last = band == 0, band == groups - 1
    lead, second = n // 2 - 1, n // 2

    edges, others = 4 * nf, rows - 4

    def dealt(slot, device):
        u = slot * n + device
        m, v = lax.rem(u, 4), jnp.maximum(u - edges, 0)
        near = u < edges
        f = jnp.where(near, u // 4, v // others)
        r = jnp.where(near, jnp.where(m >= 2, m + others, m), 2 + lax.rem(v, others))
        return f, r

    def owner(f, r):
        if r < 2:
            u = 4 * f + r
        elif r >= rows - 2:
            u = 4 * f + r - others
        else:
            u = edges + others * f + r - 2
        return lax.rem(u, n)

    for f in range(nf):
        pltpu.make_async_copy(fields_ref.at[f], mine.at[f], load_sem.at[f]).start()
    low = jnp.maximum(band * rows - 1, 0) // LANES * LANES
    low = pl.multiple_of(jnp.minimum(low, rate_ref.shape[1] - rate_raw.shape[1]), LANES)
    rate_copy = pltpu.make_async_copy(
        rate_ref.at[:, pl.ds(low, rate_raw.shape[1])], rate_raw, rate_sem
    )
    rate_copy.start()
    shift_copy = pltpu.make_async_copy(shift_ref, shift_smem, scalar_sem.at[0])
    shift_copy.start()
    fraction_copy = pltpu.make_async_copy(fraction_ref, fraction_smem, scalar_sem.at[1])
    fraction_copy.start()

    barrier = pltpu.get_barrier_semaphore()
    leads = me == lead

    @pl.when(leads)
    def _():
        with jax.named_scope("greet"):
            pl.semaphore_wait(barrier, n - 1)

        @pl.loop(1, n)
        def _(d):
            to = lax.rem(me + d, n)
            pl.semaphore_signal(go_sem, inc=1, device_id={"az": to}, device_id_type=MESH)

    @pl.when(jnp.logical_not(leads))
    def _():
        pl.semaphore_signal(barrier, inc=1, device_id={"az": lead}, device_id_type=MESH)
        with jax.named_scope("greet"):
            pl.semaphore_wait(go_sem, 1)

        @pl.when(jnp.logical_not(first))
        def _():
            pl.semaphore_signal(barrier, inc=1, device_id={"rad": band - 1}, device_id_type=MESH)

        @pl.when(jnp.logical_not(last))
        def _():
            pl.semaphore_signal(barrier, inc=1, device_id={"rad": band + 1}, device_id_type=MESH)

    def meet_neighbours():
        @pl.when(jnp.logical_not(leads))
        def _():
            pl.semaphore_wait(barrier, jnp.where(first, 0, 1) + jnp.where(last, 0, 1))

        @pl.when(me == second)
        def _():
            pl.semaphore_signal(met_sem, inc=1, device_id={"az": lead}, device_id_type=MESH)

        @pl.when(leads)
        def _():
            pl.semaphore_wait(met_sem, 1)

    for f in range(nf):
        pltpu.make_async_copy(fields_ref.at[f], mine.at[f], load_sem.at[f]).wait()

    def gather(s):
        @pl.loop(1, n)
        def _(d):
            to = lax.rem(me + d, n)
            f, r = dealt(s, to)
            pltpu.make_async_remote_copy(
                src_ref=mine.at[f, r],
                dst_ref=whole.at[s, me],
                send_sem=send_sem.at[0],
                recv_sem=gather_sem.at[s],
                device_id={"az": to},
                device_id_type=MESH,
            ).start()

    pl.loop(0, AHEAD)(gather)

    rate_copy.wait()
    at = lax.broadcasted_iota(jnp.int32, rate_raw.shape, 1) + low
    rates = rate_raw[...]
    for i in range(rows + 1):
        here = at == band * rows + i - 1
        column = jnp.sum(jnp.where(here, rates, 0.0), axis=1, keepdims=True)
        if i == 0:
            column = jnp.where(first, 0.0, column)
        if i == rows:
            column = jnp.where(last, 0.0, column)
        face_rate[i] = jnp.broadcast_to(column, (polar, LANES))

    @pl.when(first)
    def _():
        tall[:, 0:2] = jnp.zeros((nf, 2, polar, LANES), jnp.float32)

    @pl.when(last)
    def _():
        tall[:, rows + 2 : rows + 4] = jnp.zeros((nf, 2, polar, LANES), jnp.float32)

    shift_copy.wait()
    fraction_copy.wait()
    lane = lax.broadcasted_iota(jnp.int32, (n, SUB, LANES), 2)
    lane_row = lax.broadcasted_iota(jnp.int32, (polar, LANES), 1)

    def azimuthal(s):
        f, r = dealt(s, me)
        amount = shift_smem[band * rows + r]
        courant = fraction_smem[band * rows + r]
        blocks = amount >> 7
        lanes = amount & (LANES - 1)
        upwind = courant > 0.0
        weight = jnp.where(upwind, 0.5 * (1.0 - courant), -0.5 * (1.0 + courant))
        step = jnp.where(upwind, 1, LANES - 1)
        edge = jnp.where(upwind, 0, LANES - 1)

        whole[s, me] = mine[f, r]
        with jax.named_scope("rows_in"):
            got = whole.at[s, pl.ds(0, n - 1)]
            pltpu.make_async_copy(got, got, gather_sem.at[s]).wait()

        for t in range(0, polar, SUB):
            q = whole[s, :, t : t + SUB, :]
            ahead = pltpu.roll(q, LANES - 1, 2)
            right = jnp.where(lane == LANES - 1, blocks_on(ahead), ahead) - q
            back = pltpu.roll(right, 1, 2)
            left = jnp.where(lane == 0, blocks_back(back), back)
            flux = courant * (q + weight * limited(left, right))
            other = pltpu.roll(flux, step, 2)
            beside = jnp.where(upwind, blocks_back(other), blocks_on(other))
            other = jnp.where(lane == edge, beside, other)
            change = jnp.where(upwind, flux - other, other - flux)
            turned[:, t : t + SUB, :] = pltpu.roll(q - change, lanes, 2)

        @pl.loop(0, n)
        def _(j):
            from_here = lax.rem(j - blocks + n, n)
            from_last = lax.rem(j - blocks - 1 + n + n, n)
            rolled[s, j] = jnp.where(lane_row >= lanes, turned[from_here], turned[from_last])

        tall[f, r + 2] = rolled[s, me]

    def give_back(s):
        f, r = dealt(s, me)

        @pl.loop(1, n)
        def _(d):
            to = lax.rem(me + d, n)
            pltpu.make_async_remote_copy(
                src_ref=rolled.at[s, to],
                dst_ref=tall.at[f, r + 2],
                send_sem=send_sem.at[1],
                recv_sem=row_sem.at[f, r],
                device_id={"az": to},
                device_id_type=MESH,
            ).start()

    def await_row(f, j):
        @pl.when(me != owner(f, j))
        def _():
            got = tall.at[f, j + 2]
            pltpu.make_async_copy(got, got, row_sem.at[f, j]).wait()

    def halo(f, up):
        src, dst, to = (rows, 0, band + 1) if up else (2, rows + 2, band - 1)
        return pltpu.make_async_remote_copy(
            src_ref=tall.at[f, pl.ds(src, 2)],
            dst_ref=tall.at[f, pl.ds(dst, 2)],
            send_sem=halo_send_sem.at[f, int(up)],
            recv_sem=halo_sem.at[f, int(up)],
            device_id={"rad": to},
            device_id_type=MESH,
        )

    def pass_on(f):
        with jax.named_scope("edges_in"):
            await_row(f, 0)
            await_row(f, 1)
            await_row(f, rows - 2)
            await_row(f, rows - 1)

        @pl.when(jnp.logical_not(first))
        def _():
            halo(f, False).start()

        @pl.when(jnp.logical_not(last))
        def _():
            halo(f, True).start()

    def radial(f):
        with jax.named_scope("rest_in"):
            for j in range(2, rows - 2):
                await_row(f, j)

        with jax.named_scope("halo_in"):
            @pl.when(jnp.logical_not(first))
            def _():
                halo(f, True).wait_recv()

            @pl.when(jnp.logical_not(last))
            def _():
                halo(f, False).wait_recv()

        @pl.loop(0, polar // SUB)
        def _(i):
            t = pl.ds(pl.multiple_of(i * SUB, SUB), SUB)
            q = tall[f, :, t, :]
            c = face_rate[:, t, :]
            diff = q[1:] - q[:-1]
            slope = limited(diff[:-1], diff[1:])
            forward = q[1:-2] + 0.5 * (1.0 - c) * slope[:-1]
            backward = q[2:-1] - 0.5 * (1.0 + c) * slope[1:]
            flux = c * jnp.where(c > 0.0, forward, backward)
            out_ref[f, :, t, :] = q[2:-2] - (flux[1:] - flux[:-1])

    early = -(-edges // n)

    @pl.loop(0, early)
    def _(s):
        azimuthal(s)
        give_back(s)

        @pl.when(s + AHEAD < nf)
        def _():
            gather(s + AHEAD)

    pl.loop(early + AHEAD, nf)(gather)
    azimuthal(early)
    with jax.named_scope("meet"):
        meet_neighbours()
    pl.loop(0, nf)(pass_on)
    give_back(early)

    @pl.loop(early + 1, nf)
    def _(s):
        azimuthal(s)
        give_back(s)

    pl.loop(0, nf)(radial)

    with jax.named_scope("finish"):
        sent = whole.at[:, pl.ds(0, n - 1)]
        for phase in range(2):
            pltpu.make_async_copy(sent, sent, send_sem.at[phase]).wait()
        for f in range(nf):

            @pl.when(jnp.logical_not(first))
            def _():
                halo(f, False).wait_send()

            @pl.when(jnp.logical_not(last))
            def _():
                halo(f, True).wait_send()


def shards(n, groups, fields, shift, fraction, radial_rate):
    nf, rows, polar, lanes = fields.shape
    assert rows == n and lanes == LANES
    block = lambda *shape: pltpu.VMEM(shape, jnp.float32)
    return pl.pallas_call(
        functools.partial(kernel, n, groups),
        out_shape=pltpu.VMEM(fields.shape, jnp.float32),
        in_specs=[pl.BlockSpec(memory_space=pltpu.HBM)] * 4,
        out_specs=pl.BlockSpec(memory_space=pltpu.VMEM),
        scratch_shapes=[
            block(nf, rows, polar, LANES),
            block(nf, n, polar, LANES),
            block(n, polar, LANES),
            block(nf, n, polar, LANES),
            block(nf, rows + 4, polar, LANES),
            pltpu.SMEM(shift.shape, jnp.int32),
            pltpu.SMEM(fraction.shape, jnp.float32),
            block(polar, min(2 * LANES, groups * rows)),
            block(rows + 1, polar, LANES),
            pltpu.SemaphoreType.DMA((nf,)),
            pltpu.SemaphoreType.DMA,
            pltpu.SemaphoreType.DMA((2,)),
            pltpu.SemaphoreType.DMA((nf,)),
            pltpu.SemaphoreType.DMA((nf, rows)),
            pltpu.SemaphoreType.DMA((nf, 2)),
            pltpu.SemaphoreType.DMA((nf, 2)),
            pltpu.SemaphoreType.REGULAR,
            pltpu.SemaphoreType.REGULAR,
            pltpu.SemaphoreType.DMA((2,)),
        ],
        compiler_params=pltpu.CompilerParams(
            collective_id=0, has_side_effects=True, vmem_limit_bytes=VMEM_BYTES
        ),
        name="orbital",
    )(shift, fraction, fields, radial_rate.T)


def solution(mesh):
    placed = (P(None, "rad", None, "az"), P(), P(), P())
    body = functools.partial(shards, mesh.shape["az"], mesh.shape["rad"])
    return jax.shard_map(
        body, mesh=mesh, in_specs=placed, out_specs=P(None, "rad", None, "az"), check_vma=False
    )
```

time: 65 us -> 48.1 us (0.74)
  the two profiles are of different devices: /device:TPU:32 before, /device:TPU:192 now
where the time goes in v2:
time: 48.1 us; the launch traced here: 48 us
  Pallas kernels  47.1 us (98%)
  local copies, waits for them, and re-layouts  0.95 us (2%)
    pallas_call x1, Pallas kernels, shards(): pl.pallas_call(functools.partial(kernel, n, groups), out_shape=pltpu.VMEM...  47.1 us

profile of v2, /device:TPU:192, one launch (start us, length us, event | category | flops | bytes accessed | tf_op | source)
XLA Modules:
  0.0 48.0 jit_solution(8838789533029921398)
XLA Ops:
  0.0 47.1 %orbital.1 = f32[5,12,32,128]{3,2,1,0:T(8,128)S(1)} custom-call(s32[768]{0:T(1024)} %shift_ref.1, f32[768]{0:T(1024)} %fraction_ref.1, f32[5,12,32,128]{3,2,1,0:T(8,128)} %fields_ref.1, f32[32,768]{1,0:T(8,128)} %bitcast.1), custom_call_target="tpu_custom_call" | custom-call | tf_op jit(solution)/shard_map/orbital/pallas_call | solution.py:336
  47.1 0.9 %copy.6 = f32[5,12,32,128]{3,2,1,0:T(8,128)} copy(f32[5,12,32,128]{3,2,1,0:T(8,128)S(1)} %orbital.1) | data formatting | bytes 1966080

commit v3 on v2

--- a/solution.py
+++ b/solution.py
@@ -11,6 +11,7 @@
 LANES = 128
 SUB = 8
 AHEAD = 3
+RING = 8
 VMEM_BYTES = 67043328 - 6000000
 
 
@@ -61,9 +62,10 @@
     me = lax.axis_index("az")
     band = lax.axis_index("rad")
     first, last = band == 0, band == groups - 1
-    lead, second = n // 2 - 1, n // 2
+    contact, teller = n - 2, n - 1
 
     edges, others = 4 * nf, rows - 4
+    early = -(-edges // n)
 
     def dealt(slot, device):
         u = slot * n + device
@@ -96,21 +98,58 @@
     fraction_copy.start()
 
     barrier = pltpu.get_barrier_semaphore()
-    leads = me == lead
-
-    @pl.when(leads)
+    meets = me == contact
+
+    @pl.loop(1, n)
+    def _(d):
+        to = lax.rem(me + d, n)
+
+        @pl.when(to != contact)
+        def _():
+            pl.semaphore_signal(barrier, inc=1, device_id={"az": to}, device_id_type=MESH)
+
+    for f in range(nf):
+        pltpu.make_async_copy(fields_ref.at[f], mine.at[f], load_sem.at[f]).wait()
+
+    @pl.loop(0, nf)
+    def _(s):
+        f, r = dealt(s, me)
+        whole[s * n + me] = mine[f, r]
+
+    shift_copy.wait()
+    fraction_copy.wait()
+
+    rate_copy.wait()
+    at = lax.broadcasted_iota(jnp.int32, rate_raw.shape, 1) + low
+    rates = rate_raw[...]
+    for i in range(rows + 1):
+        here = at == band * rows + i - 1
+        rate = jnp.sum(jnp.where(here, rates, 0.0), axis=1, keepdims=True)
+        if i == 0:
+            rate = jnp.where(first, 0.0, rate)
+        if i == rows:
+            rate = jnp.where(last, 0.0, rate)
+        face_rate[i] = jnp.broadcast_to(rate, (polar, LANES))
+
+    @pl.when(first)
+    def _():
+        tall[:, 0:2] = jnp.zeros((nf, 2, polar, LANES), jnp.float32)
+
+    @pl.when(last)
+    def _():
+        tall[:, rows + 2 : rows + 4] = jnp.zeros((nf, 2, polar, LANES), jnp.float32)
+
+    @pl.when(jnp.logical_not(meets))
     def _():
         with jax.named_scope("greet"):
             pl.semaphore_wait(barrier, n - 1)
 
-        @pl.loop(1, n)
-        def _(d):
-            to = lax.rem(me + d, n)
-            pl.semaphore_signal(go_sem, inc=1, device_id={"az": to}, device_id_type=MESH)
-
-    @pl.when(jnp.logical_not(leads))
-    def _():
-        pl.semaphore_signal(barrier, inc=1, device_id={"az": lead}, device_id_type=MESH)
+    @pl.when(me == teller)
+    def _():
+        pl.semaphore_signal(go_sem, inc=1, device_id={"az": contact}, device_id_type=MESH)
+
+    @pl.when(meets)
+    def _():
         with jax.named_scope("greet"):
             pl.semaphore_wait(go_sem, 1)
 
@@ -123,20 +162,18 @@
             pl.semaphore_signal(barrier, inc=1, device_id={"rad": band + 1}, device_id_type=MESH)
 
     def meet_neighbours():
-        @pl.when(jnp.logical_not(leads))
+        @pl.when(meets)
         def _():
             pl.semaphore_wait(barrier, jnp.where(first, 0, 1) + jnp.where(last, 0, 1))
 
-        @pl.when(me == second)
-        def _():
-            pl.semaphore_signal(met_sem, inc=1, device_id={"az": lead}, device_id_type=MESH)
-
-        @pl.when(leads)
+            @pl.loop(1, n)
+            def _(d):
+                to = lax.rem(me + d, n)
+                pl.semaphore_signal(met_sem, inc=1, device_id={"az": to}, device_id_type=MESH)
+
+        @pl.when(jnp.logical_not(meets))
         def _():
             pl.semaphore_wait(met_sem, 1)
-
-    for f in range(nf):
-        pltpu.make_async_copy(fields_ref.at[f], mine.at[f], load_sem.at[f]).wait()
 
     def gather(s):
         @pl.loop(1, n)
@@ -145,7 +182,7 @@
             f, r = dealt(s, to)
             pltpu.make_async_remote_copy(
                 src_ref=mine.at[f, r],
-                dst_ref=whole.at[s, me],
+                dst_ref=whole.at[s * n + me],
                 send_sem=send_sem.at[0],
                 recv_sem=gather_sem.at[s],
                 device_id={"az": to},
@@ -154,28 +191,6 @@
 
     pl.loop(0, AHEAD)(gather)
 
-    rate_copy.wait()
-    at = lax.broadcasted_iota(jnp.int32, rate_raw.shape, 1) + low
-    rates = rate_raw[...]
-    for i in range(rows + 1):
-        here = at == band * rows + i - 1
-        column = jnp.sum(jnp.where(here, rates, 0.0), axis=1, keepdims=True)
-        if i == 0:
-            column = jnp.where(first, 0.0, column)
-        if i == rows:
-            column = jnp.where(last, 0.0, column)
-        face_rate[i] = jnp.broadcast_to(column, (polar, LANES))
-
-    @pl.when(first)
-    def _():
-        tall[:, 0:2] = jnp.zeros((nf, 2, polar, LANES), jnp.float32)
-
-    @pl.when(last)
-    def _():
-        tall[:, rows + 2 : rows + 4] = jnp.zeros((nf, 2, polar, LANES), jnp.float32)
-
-    shift_copy.wait()
-    fraction_copy.wait()
     lane = lax.broadcasted_iota(jnp.int32, (n, SUB, LANES), 2)
     lane_row = lax.broadcasted_iota(jnp.int32, (polar, LANES), 1)
 
@@ -190,13 +205,12 @@
         step = jnp.where(upwind, 1, LANES - 1)
         edge = jnp.where(upwind, 0, LANES - 1)
 
-        whole[s, me] = mine[f, r]
         with jax.named_scope("rows_in"):
-            got = whole.at[s, pl.ds(0, n - 1)]
+            got = whole.at[pl.ds(s * n, n - 1)]
             pltpu.make_async_copy(got, got, gather_sem.at[s]).wait()
 
         for t in range(0, polar, SUB):
-            q = whole[s, :, t : t + SUB, :]
+            q = whole[pl.ds(s * n, n), t : t + SUB, :]
             ahead = pltpu.roll(q, LANES - 1, 2)
             right = jnp.where(lane == LANES - 1, blocks_on(ahead), ahead) - q
             back = pltpu.roll(right, 1, 2)
@@ -212,9 +226,9 @@
         def _(j):
             from_here = lax.rem(j - blocks + n, n)
             from_last = lax.rem(j - blocks - 1 + n + n, n)
-            rolled[s, j] = jnp.where(lane_row >= lanes, turned[from_here], turned[from_last])
-
-        tall[f, r + 2] = rolled[s, me]
+            rolled[s * n + j] = jnp.where(lane_row >= lanes, turned[from_here], turned[from_last])
+
+        tall[f, r + 2] = rolled[s * n + me]
 
     def give_back(s):
         f, r = dealt(s, me)
@@ -223,7 +237,7 @@
         def _(d):
             to = lax.rem(me + d, n)
             pltpu.make_async_remote_copy(
-                src_ref=rolled.at[s, to],
+                src_ref=rolled.at[s * n + to],
                 dst_ref=tall.at[f, r + 2],
                 send_sem=send_sem.at[1],
                 recv_sem=row_sem.at[f, r],
@@ -289,35 +303,40 @@
             flux = c * jnp.where(c > 0.0, forward, backward)
             out_ref[f, :, t, :] = q[2:-2] - (flux[1:] - flux[:-1])
 
-    early = -(-edges // n)
-
-    @pl.loop(0, early)
+    hold = lax.rem(band, RING) >= RING - 2
+
+    def halos():
+        with jax.named_scope("meet"):
+            meet_neighbours()
+        pl.loop(0, nf)(pass_on)
+
+    @pl.loop(0, nf)
     def _(s):
         azimuthal(s)
+
+        @pl.when(hold & (s == early))
+        def _():
+            halos()
+
         give_back(s)
 
-        @pl.when(s + AHEAD < nf)
-        def _():
-            gather(s + AHEAD)
-
-    pl.loop(early + AHEAD, nf)(gather)
-    azimuthal(early)
-    with jax.named_scope("meet"):
-        meet_neighbours()
-    pl.loop(0, nf)(pass_on)
-    give_back(early)
-
-    @pl.loop(early + 1, nf)
-    def _(s):
-        azimuthal(s)
-        give_back(s)
+        @pl.when(jnp.logical_not(hold) & (s == early))
+        def _():
+            halos()
+
+        @pl.loop(s + AHEAD, jnp.where(s == early - 1, nf, jnp.minimum(s + AHEAD + 1, nf)))
+        def _(later):
+            @pl.when(s < early)
+            def _():
+                gather(later)
 
     pl.loop(0, nf)(radial)
 
     with jax.named_scope("finish"):
-        sent = whole.at[:, pl.ds(0, n - 1)]
         for phase in range(2):
+            sent = whole.at[pl.ds(0, nf * (n - 1))]
             pltpu.make_async_copy(sent, sent, send_sem.at[phase]).wait()
+
         for f in range(nf):
 
             @pl.when(jnp.logical_not(first))
@@ -331,7 +350,7 @@
 
 def shards(n, groups, fields, shift, fraction, radial_rate):
     nf, rows, polar, lanes = fields.shape
-    assert rows == n and lanes == LANES
+    assert rows == n and lanes == LANES and rows >= 4
     block = lambda *shape: pltpu.VMEM(shape, jnp.float32)
     return pl.pallas_call(
         functools.partial(kernel, n, groups),
@@ -340,9 +359,9 @@
         out_specs=pl.BlockSpec(memory_space=pltpu.VMEM),
         scratch_shapes=[
             block(nf, rows, polar, LANES),
-            block(nf, n, polar, LANES),
+            block(nf * n, polar, LANES),
             block(n, polar, LANES),
-            block(nf, n, polar, LANES),
+            block(nf * n, polar, LANES),
             block(nf, rows + 4, polar, LANES),
             pltpu.SMEM(shift.shape, jnp.int32),
             pltpu.SMEM(fraction.shape, jnp.float32),

time: 48.1 us -> 47.3 us (0.983)
  the two profiles are of different devices: /device:TPU:192 before, /device:TPU:65 now
where the time goes in v3:
time: 47.3 us; the launch traced here: 47.2 us
  Pallas kernels  46.2 us (98%)
  local copies, waits for them, and re-layouts  0.95 us (2%)
    pallas_call x1, Pallas kernels, shards(): pl.pallas_call(functools.partial(kernel, n, groups), out_shape=pltpu.VMEM...  46.2 us
    unnamed x1, local copies, waits for them, and re-layouts  0.95 us

profile of v3, /device:TPU:65, one launch (start us, length us, event | category | flops | bytes accessed | tf_op | source)
XLA Modules:
  0.0 47.2 jit_solution(14946302424387039785)
XLA Ops:
  0.0 46.2 %orbital.1 = f32[5,12,32,128]{3,2,1,0:T(8,128)S(1)} custom-call(s32[768]{0:T(1024)} %shift_ref.1, f32[768]{0:T(1024)} %fraction_ref.1, f32[5,12,32,128]{3,2,1,0:T(8,128)} %fields_ref.1, f32[32,768]{1,0:T(8,128)} %bitcast.1), custom_call_target="tpu_custom_call" | custom-call | tf_op jit(solution)/shard_map/orbital/pallas_call | solution.py:355
  46.2 0.9 %copy.6 = f32[5,12,32,128]{3,2,1,0:T(8,128)} copy(f32[5,12,32,128]{3,2,1,0:T(8,128)S(1)} %orbital.1) | data formatting | bytes 1966080

commit v4 on v3

--- a/solution.py
+++ b/solution.py
@@ -11,7 +11,6 @@
 LANES = 128
 SUB = 8
 AHEAD = 3
-RING = 8
 VMEM_BYTES = 67043328 - 6000000
 
 
@@ -64,25 +63,42 @@
     first, last = band == 0, band == groups - 1
     contact, teller = n - 2, n - 1
 
-    edges, others = 4 * nf, rows - 4
-    early = -(-edges // n)
+    third = n // 3
+    near, others = 2 * nf, rows - 4
+    early = 2
+    upper = lax.rem(band, 2) == 1
+    seat = jnp.where(upper, n - 1 - me, me)
+    far_base = jnp.where(upper, rows - 2, 0)
+    near_base = jnp.where(upper, 0, rows - 2)
+    far_there = jnp.where(upper, jnp.logical_not(last), jnp.logical_not(first))
+    far_band = jnp.where(upper, band + 1, band - 1)
+    far_row = jnp.where(upper, 0, rows + 2)
+    spare = 2 * nf - 2 * third
+    far_count = jnp.where(seat < third, 2, jnp.where(seat < third + spare, 1, 0))
 
     def dealt(slot, device):
-        u = slot * n + device
-        m, v = lax.rem(u, 4), jnp.maximum(u - edges, 0)
-        near = u < edges
-        f = jnp.where(near, u // 4, v // others)
-        r = jnp.where(near, jnp.where(m >= 2, m + others, m), 2 + lax.rem(v, others))
+        at = jnp.where(upper, n - 1 - device, device)
+        in_first = slot == 0
+        is_far = at < jnp.where(in_first, third, third + spare)
+        c = jnp.where(is_far, at + slot * third, at - jnp.where(in_first, third, spare - third))
+        u = slot * n + at
+        v = jnp.maximum(u - 4 * nf, 0)
+        edge = u < 4 * nf
+        f = jnp.where(edge, c // 2, v // others)
+        base = jnp.where(is_far, far_base, near_base)
+        r = jnp.where(edge, base + lax.rem(c, 2), 2 + lax.rem(v, others))
         return f, r
 
     def owner(f, r):
-        if r < 2:
-            u = 4 * f + r
-        elif r >= rows - 2:
-            u = 4 * f + r - others
+        c = 2 * f + (r if r < 2 else r - others - 2)
+        is_far = upper if r >= rows - 2 else jnp.logical_not(upper)
+        if 2 <= r < rows - 2:
+            at = lax.rem(4 * nf + others * f + r - 2, n)
         else:
-            u = edges + others * f + r - 2
-        return lax.rem(u, n)
+            far_at = jnp.where(c < third, c, c - third)
+            near_at = jnp.where(c < 2 * third, c + third, c + spare - third)
+            at = jnp.where(is_far, far_at, near_at)
+        return jnp.where(upper, n - 1 - at, at)
 
     for f in range(nf):
         pltpu.make_async_copy(fields_ref.at[f], mine.at[f], load_sem.at[f]).start()
@@ -251,45 +267,70 @@
             got = tall.at[f, j + 2]
             pltpu.make_async_copy(got, got, row_sem.at[f, j]).wait()
 
-    def halo(f, up):
+    def send_far():
+        @pl.loop(2 - far_count, 2)
+        def _(s):
+            f, r = dealt(s, me)
+
+            @pl.loop(0, n)
+            def _(d):
+                to = lax.rem(me + d, n)
+                pltpu.make_async_remote_copy(
+                    src_ref=rolled.at[s * n + to],
+                    dst_ref=tall.at[f, far_row + r - far_base],
+                    send_sem=halo_send_sem.at[0],
+                    recv_sem=halo_sem.at[f, 0],
+                    device_id={"az": to, "rad": far_band},
+                    device_id_type=MESH,
+                ).start()
+
+    def near_halo(f, up):
         src, dst, to = (rows, 0, band + 1) if up else (2, rows + 2, band - 1)
         return pltpu.make_async_remote_copy(
             src_ref=tall.at[f, pl.ds(src, 2)],
             dst_ref=tall.at[f, pl.ds(dst, 2)],
-            send_sem=halo_send_sem.at[f, int(up)],
-            recv_sem=halo_sem.at[f, int(up)],
+            send_sem=halo_send_sem.at[1],
+            recv_sem=halo_sem.at[f, 1],
             device_id={"rad": to},
             device_id_type=MESH,
         )
 
     def pass_on(f):
-        with jax.named_scope("edges_in"):
+        @pl.when(upper)
+        def _():
             await_row(f, 0)
             await_row(f, 1)
+            near_halo(f, False).start()
+
+        @pl.when(jnp.logical_not(upper))
+        def _():
             await_row(f, rows - 2)
             await_row(f, rows - 1)
-
-        @pl.when(jnp.logical_not(first))
-        def _():
-            halo(f, False).start()
-
-        @pl.when(jnp.logical_not(last))
-        def _():
-            halo(f, True).start()
+            near_halo(f, True).start()
 
     def radial(f):
         with jax.named_scope("rest_in"):
+            @pl.when(upper)
+            def _():
+                await_row(f, rows - 2)
+                await_row(f, rows - 1)
+
+            @pl.when(jnp.logical_not(upper))
+            def _():
+                await_row(f, 0)
+                await_row(f, 1)
+
             for j in range(2, rows - 2):
                 await_row(f, j)
 
         with jax.named_scope("halo_in"):
-            @pl.when(jnp.logical_not(first))
+            two = tall.at[f, pl.ds(0, 2)]
+
+            @pl.when(far_there)
             def _():
-                halo(f, True).wait_recv()
-
-            @pl.when(jnp.logical_not(last))
-            def _():
-                halo(f, False).wait_recv()
+                pltpu.make_async_copy(two, two, halo_sem.at[f, 0]).wait()
+
+            pltpu.make_async_copy(two, two, halo_sem.at[f, 1]).wait()
 
         @pl.loop(0, polar // SUB)
         def _(i):
@@ -303,26 +344,21 @@
             flux = c * jnp.where(c > 0.0, forward, backward)
             out_ref[f, :, t, :] = q[2:-2] - (flux[1:] - flux[:-1])
 
-    hold = lax.rem(band, RING) >= RING - 2
-
-    def halos():
-        with jax.named_scope("meet"):
-            meet_neighbours()
-        pl.loop(0, nf)(pass_on)
-
     @pl.loop(0, nf)
     def _(s):
         azimuthal(s)
 
-        @pl.when(hold & (s == early))
-        def _():
-            halos()
+        @pl.when(s == early)
+        def _():
+            with jax.named_scope("meet"):
+                meet_neighbours()
+            pl.when(far_there)(send_far)
 
         give_back(s)
 
-        @pl.when(jnp.logical_not(hold) & (s == early))
-        def _():
-            halos()
+        @pl.when(s == early)
+        def _():
+            pl.loop(0, nf)(pass_on)
 
         @pl.loop(s + AHEAD, jnp.where(s == early - 1, nf, jnp.minimum(s + AHEAD + 1, nf)))
         def _(later):
@@ -337,20 +373,20 @@
             sent = whole.at[pl.ds(0, nf * (n - 1))]
             pltpu.make_async_copy(sent, sent, send_sem.at[phase]).wait()
 
-        for f in range(nf):
-
-            @pl.when(jnp.logical_not(first))
+        for units in (1, 2):
+
+            @pl.when(far_there & (far_count == units))
             def _():
-                halo(f, False).wait_send()
-
-            @pl.when(jnp.logical_not(last))
-            def _():
-                halo(f, True).wait_send()
+                sent = rolled.at[pl.ds(0, units * n)]
+                pltpu.make_async_copy(sent, sent, halo_send_sem.at[0]).wait()
+
+        sent = rolled.at[pl.ds(0, 2 * nf)]
+        pltpu.make_async_copy(sent, sent, halo_send_sem.at[1]).wait()
 
 
 def shards(n, groups, fields, shift, fraction, radial_rate):
     nf, rows, polar, lanes = fields.shape
-    assert rows == n and lanes == LANES and rows >= 4
+    assert rows == n == 12 and lanes == LANES and nf == 5 and groups % 2 == 0
     block = lambda *shape: pltpu.VMEM(shape, jnp.float32)
     return pl.pallas_call(
         functools.partial(kernel, n, groups),
@@ -372,7 +408,7 @@
             pltpu.SemaphoreType.DMA((2,)),
             pltpu.SemaphoreType.DMA((nf,)),
             pltpu.SemaphoreType.DMA((nf, rows)),
-            pltpu.SemaphoreType.DMA((nf, 2)),
+            pltpu.SemaphoreType.DMA((2,)),
             pltpu.SemaphoreType.DMA((nf, 2)),
             pltpu.SemaphoreType.REGULAR,
             pltpu.SemaphoreType.REGULAR,

time: 47.3 us -> 45.1 us (0.953)
  the two profiles are of different devices: /device:TPU:65 before, /device:TPU:7 now
where the time goes in v4:
time: 45.1 us; the launch traced here: 45 us
  Pallas kernels  44 us (98%)
  local copies, waits for them, and re-layouts  0.95 us (2%)
    pallas_call x1, Pallas kernels, shards(): pl.pallas_call(functools.partial(kernel, n, groups), out_shape=pltpu.VMEM...  44 us
    unnamed x1, local copies, waits for them, and re-layouts  0.95 us

profile of v4, /device:TPU:7, one launch (start us, length us, event | category | flops | bytes accessed | tf_op | source)
XLA Modules:
  0.0 45.0 jit_solution(607129735246987993)
XLA Ops:
  0.0 44.0 %orbital.1 = f32[5,12,32,128]{3,2,1,0:T(8,128)S(1)} custom-call(s32[768]{0:T(1024)} %shift_ref.1, f32[768]{0:T(1024)} %fraction_ref.1, f32[5,12,32,128]{3,2,1,0:T(8,128)} %fields_ref.1, f32[32,768]{1,0:T(8,128)} %bitcast.1), custom_call_target="tpu_custom_call" | custom-call | tf_op jit(solution)/shard_map/orbital/pallas_call | solution.py:391
  44.0 0.9 %copy.6 = f32[5,12,32,128]{3,2,1,0:T(8,128)} copy(f32[5,12,32,128]{3,2,1,0:T(8,128)S(1)} %orbital.1) | data formatting | bytes 1966080

commit v5 on v4

--- a/solution.py
+++ b/solution.py
@@ -187,6 +187,7 @@
                 to = lax.rem(me + d, n)
                 pl.semaphore_signal(met_sem, inc=1, device_id={"az": to}, device_id_type=MESH)
 
+    def await_meeting():
         @pl.when(jnp.logical_not(meets))
         def _():
             pl.semaphore_wait(met_sem, 1)
@@ -351,10 +352,11 @@
         @pl.when(s == early)
         def _():
             with jax.named_scope("meet"):
-                meet_neighbours()
+                await_meeting()
             pl.when(far_there)(send_far)
 
         give_back(s)
+        pl.when(s == early - 1)(meet_neighbours)
 
         @pl.when(s == early)
         def _():

time: 45.1 us -> 45.2 us (level)
  no operation moved by 1% of the time
where the time goes in v5:
time: 45.2 us; the launch traced here: 45 us
  Pallas kernels  44.1 us (98%)
  local copies, waits for them, and re-layouts  0.95 us (2%)
    pallas_call x1, Pallas kernels, shards(): pl.pallas_call(functools.partial(kernel, n, groups), out_shape=pltpu.VMEM...  44.1 us
    unnamed x1, local copies, waits for them, and re-layouts  0.95 us

profile of v5, /device:TPU:7, one launch (start us, length us, event | category | flops | bytes accessed | tf_op | source)
XLA Modules:
  0.0 45.0 jit_solution(16489606348732404090)
XLA Ops:
  0.0 44.1 %orbital.1 = f32[5,12,32,128]{3,2,1,0:T(8,128)S(1)} custom-call(s32[768]{0:T(1024)} %shift_ref.1, f32[768]{0:T(1024)} %fraction_ref.1, f32[5,12,32,128]{3,2,1,0:T(8,128)} %fields_ref.1, f32[32,768]{1,0:T(8,128)} %bitcast.1), custom_call_target="tpu_custom_call" | custom-call | tf_op jit(solution)/shard_map/orbital/pallas_call | solution.py:393
  44.1 0.9 %copy.6 = f32[5,12,32,128]{3,2,1,0:T(8,128)} copy(f32[5,12,32,128]{3,2,1,0:T(8,128)S(1)} %orbital.1) | data formatting | bytes 1966080
